TPU v7x, 32 devices: a whole 2x2x4 slice. The times are simulated.
32 devices in a mesh: slab: 2 (over x), row: 16 (over z, y, core).
Axes of the slice: x: 2, y: 2, z: 4, core: 2. Of those that a mesh axis runs over, the one named last changes fastest.
Arguments:
- raw_echo: float32 [2, 1024, 16384], P(None, 'slab', 'row'), parts along dimension 1, may hold values from -6 to 6
- centroid: int32 [8], P('slab'), parts along dimension 0, may hold values from 0 to 16383
- shifts: int32 [8], P('slab'), parts along dimension 0, may hold values from 0 to 12, as said below
- chirp_rate: float32 [1024], P(('slab', 'row')), parts along dimension 0, may hold values from 50 to 400
Outputs:
- focused_image: float32 [2, 1024, 16384], P(None, ('slab', 'row')), parts along dimension 1
There are 2 independent parts, one for each index of `slab`. A program takes and returns all parts, laid end to end along the dimension named above; each array names one. Nothing has to cross between parts.
Inputs may be any that keep to these rules, and one draw needn't show every extreme that they name: `shifts`: range migration of each block in range bins; some block reaches 12 in every draw.
All inputs are finite; a program needn't handle non-finite values.
Results may differ from a plain program's by a relative error of at most 0.0003.
Values sent between devices are 32-bit elements; how exact they have to be, the bound alone decides.
A program may use at most 128 MiB of HBM per device.

v0:
```python
import functools
import math

import jax
import jax.numpy as jnp
import numpy as np
from jax import lax
from jax.experimental import pallas as pl
from jax.experimental.pallas import tpu as pltpu
from jax.sharding import PartitionSpec as P

FACTOR = 128
PULSES = FACTOR * FACTOR
BLOCK = 128
MAXSHIFT = 12
TAPS = 4
LOWER = TAPS - 1
UPPER = MAXSHIFT + TAPS - 1
GROUP = 8
SUB = 8


def split(value):
    high = value.astype(jnp.bfloat16)
    low = (value - high.astype(jnp.float32)).astype(jnp.bfloat16)
    return high, low


def tables(inverse):
    grid = np.outer(np.arange(FACTOR), np.arange(FACTOR)).astype(np.float64)
    angle = 2.0 * math.pi * (grid % FACTOR) / FACTOR
    scale = 1.0 / FACTOR if inverse else 1.0
    cosine = np.cos(angle) * scale
    sine = np.sin(angle) * scale * (-1.0 if inverse else 1.0)
    left = np.block([[cosine, sine], [-sine, cosine]]).astype(np.float32)
    right = np.block([[cosine, -sine], [sine, cosine]]).astype(np.float32)
    turn = 2.0 * math.pi * grid / PULSES
    twist = np.stack([np.cos(turn), np.sin(turn) * (1.0 if inverse else -1.0)]).astype(np.float32)

    def pieces(table):
        high = table.astype(jnp.bfloat16)
        low = (table - high.astype(np.float32)).astype(jnp.bfloat16)
        return high, low

    left_high, left_low = pieces(left)
    right_high, right_low = pieces(right)
    left_all = np.concatenate([left_high, left_high, left_low], axis=1)
    right_all = np.concatenate([right_high, right_high, right_low], axis=0)
    return jnp.asarray(left_all), jnp.asarray(right_all), jnp.asarray(twist)


def left_product(left_ref, first, second):
    operand = jnp.concatenate(
        [jnp.concatenate([first[0], second[0]], axis=1), jnp.concatenate([first[1], second[1]], axis=1)],
        axis=0,
    )
    high, low = split(operand)
    stacked = jnp.concatenate([high, low, high], axis=0)
    return jnp.dot(left_ref[...], stacked, preferred_element_type=jnp.float32)


def right_product(right_ref, operand):
    high, low = split(operand)
    stacked = jnp.concatenate([high, low, high], axis=1)
    return jnp.dot(stacked, right_ref[...], preferred_element_type=jnp.float32)


def turned(real, imag, twist_ref):
    return real * twist_ref[0] - imag * twist_ref[1], real * twist_ref[1] + imag * twist_ref[0]


def forward_pair(rows, left_ref, right_ref, twist_ref):
    product = left_product(left_ref, rows[0], rows[1])
    parts = []
    for k in range(2):
        lanes = slice(k * FACTOR, (k + 1) * FACTOR)
        real, imag = turned(product[:FACTOR, lanes], product[FACTOR:, lanes], twist_ref)
        parts.append(jnp.concatenate([real, imag], axis=1))
    return right_product(right_ref, jnp.concatenate(parts, axis=0))


def forward_kernel(x_ref, left_ref, right_ref, twist_ref, out_ref, slow):
    sources = x_ref.shape[1]
    pieces = x_ref.shape[3] // FACTOR
    for c in range(2):
        for d in range(sources):
            for j in range(pieces):
                start = (d * pieces + j) * GROUP
                slow[c, start : start + GROUP, :] = x_ref[c, d, :, j * FACTOR : (j + 1) * FACTOR]
    for r in range(0, GROUP, 2):
        rows = [
            [slow[c, pl.ds(r + k, FACTOR, stride=GROUP), :] for c in range(2)] for k in range(2)
        ]
        result = forward_pair(rows, left_ref, right_ref, twist_ref)
        for k in range(2):
            part = result[k * FACTOR : (k + 1) * FACTOR]
            out_ref[0, r + k] = part[:, :FACTOR]
            out_ref[1, r + k] = part[:, FACTOR:]


def half_turns(t):
    n = jnp.round(t)
    w = (t - n) * math.pi
    odd = n - 2.0 * jnp.floor(n * 0.5)
    sign = 1.0 - 2.0 * odd
    w2 = w * w
    sine = w * (1.0 + w2 * (-1 / 6 + w2 * (1 / 120 + w2 * (-1 / 5040 + w2 * (1 / 362880 - w2 * (1 / 39916800))))))
    cosine = 1.0 + w2 * (-0.5 + w2 * (1 / 24 + w2 * (-1 / 720 + w2 * (1 / 40320 - w2 * (1 / 3628800)))))
    return sign, sine, cosine


def relative_of(start, center):
    slow = lax.broadcasted_iota(jnp.int32, (SUB, FACTOR), 0) + start
    fast = lax.broadcasted_iota(jnp.int32, (SUB, FACTOR), 1)
    bins = fast * FACTOR + slow
    wrapped = ((bins - center + PULSES // 2) & (PULSES - 1)) - PULSES // 2
    return wrapped.astype(jnp.float32) * (1.0 / PULSES)


def fill_weights(center, shift, weights, window):
    @pl.loop(0, FACTOR // SUB)
    def _(q):
        start = pl.multiple_of(q * SUB, SUB)
        relative = relative_of(start, center)
        squared = relative * relative
        migration = shift.astype(jnp.float32) * 4.0 * squared
        sign, sine, _c = half_turns(migration)
        sine = sign * sine
        sign4, sine4, cosine4 = half_turns(migration * 0.25)
        sine4 = sign4 * sine4
        cosine4 = sign4 * cosine4
        for s in range(-LOWER, UPPER + 1):
            x = s - migration
            zero = x == 0.0
            numerator = sine * ((1.0 if s % 2 else -1.0) / math.pi)
            sinc = jnp.where(zero, 1.0, numerator / jnp.where(zero, 1.0, x))
            taper = 0.5 + (0.5 * math.cos(math.pi * s / 4)) * cosine4 + (0.5 * math.sin(math.pi * s / 4)) * sine4
            value = jnp.where(jnp.abs(x) < TAPS, sinc * taper, 0.0)
            weights[s + LOWER, pl.ds(start, SUB), :] = value
        wsign, _s, wcos = half_turns(2.0 * relative)
        window[0, pl.ds(start, SUB), :] = 0.54 + 0.46 * (wsign * wcos)
        window[1, pl.ds(start, SUB), :] = squared


def migrate_rows(base, extended, rates_ref, rate_base, weights, window, focus):
    @pl.loop(0, FACTOR // SUB)
    def _(q):
        here = pl.ds(pl.multiple_of(q * SUB, SUB), SUB)
        sums = []
        for c in range(2):
            for r in range(GROUP):
                total = weights[0, here, :] * extended[c, base + r, here, :]
                for s in range(1, LOWER + UPPER + 1):
                    total = total + weights[s, here, :] * extended[c, base + r + s, here, :]
                sums.append(total)
        shape = window[0, here, :]
        squared = window[1, here, :]
        for r in range(GROUP):
            sign, sine, cosine = half_turns(rates_ref[rate_base + r] * squared)
            gain = sign * shape
            real, imag = sums[r] * gain, sums[GROUP + r] * gain
            focus[r, here, :FACTOR] = real * cosine + imag * sine
            focus[r, here, FACTOR:] = imag * cosine - real * sine


def inverse_group(focus, left_ref, right_ref, twist_ref, slow, out_ref):
    for r in range(0, GROUP, 2):
        operand = jnp.concatenate([focus[r], focus[r + 1]], axis=0)
        product = right_product(right_ref, operand)
        rows = []
        for k in range(2):
            part = product[k * FACTOR : (k + 1) * FACTOR]
            rows.append(turned(part[:, :FACTOR], part[:, FACTOR:], twist_ref))
        result = left_product(left_ref, rows[0], rows[1])
        for k in range(2):
            lanes = slice(k * FACTOR, (k + 1) * FACTOR)
            for c in range(2):
                slow[c, pl.ds(r + k, FACTOR, stride=GROUP), :] = result[c * FACTOR : (c + 1) * FACTOR, lanes]
    for c in range(2):
        for n in range(FACTOR):
            out_ref[c, :, n * FACTOR : (n + 1) * FACTOR] = slow[c, n * GROUP : (n + 1) * GROUP, :]


def backward_kernel(
    place_ref, rates_ref, own_ref, above_ref, below_ref, left_ref, right_ref, twist_ref,
    out_ref, extended, weights, window, focus, slow, sems,
):
    step = pl.program_id(0)
    own_rows = own_ref.shape[1]

    @pl.when(step == 0)
    def _():
        copies = [
            pltpu.make_async_copy(below_ref, extended.at[:, 0:LOWER], sems.at[0]),
            pltpu.make_async_copy(own_ref, extended.at[:, LOWER : LOWER + own_rows], sems.at[1]),
            pltpu.make_async_copy(above_ref, extended.at[:, LOWER + own_rows : LOWER + own_rows + UPPER], sems.at[2]),
        ]
        for copy in copies:
            copy.start()
        fill_weights(place_ref[0], place_ref[1], weights, window)
        for copy in copies:
            copy.wait()

    base = step * GROUP
    migrate_rows(base, extended, rates_ref, base, weights, window, focus)
    inverse_group(focus, left_ref, right_ref, twist_ref, slow, out_ref)


def backward(place, rates, own, above, below):
    own_rows = own.shape[1]
    left, right, twist = tables(True)
    vmem = pl.BlockSpec(memory_space=pltpu.VMEM)
    smem = pl.BlockSpec(memory_space=pltpu.SMEM)
    hbm = pl.BlockSpec(memory_space=pl.ANY)
    return pl.pallas_call(
        backward_kernel,
        grid=(own_rows // GROUP,),
        in_specs=[smem, smem, hbm, hbm, hbm, vmem, vmem, vmem],
        out_specs=pl.BlockSpec((2, GROUP, PULSES), lambda g: (0, g, 0)),
        out_shape=jax.ShapeDtypeStruct((2, own_rows, PULSES), jnp.float32),
        scratch_shapes=[
            pltpu.VMEM((2, own_rows + LOWER + UPPER, FACTOR, FACTOR), jnp.float32),
            pltpu.VMEM((LOWER + UPPER + 1, FACTOR, FACTOR), jnp.float32),
            pltpu.VMEM((2, FACTOR, FACTOR), jnp.float32),
            pltpu.VMEM((GROUP, FACTOR, 2 * FACTOR), jnp.float32),
            pltpu.VMEM((2, FACTOR * GROUP, FACTOR), jnp.float32),
            pltpu.SemaphoreType.DMA((3,)),
        ],
        compiler_params=pltpu.CompilerParams(vmem_limit_bytes=40 * 2**20),
    )(place, rates, own, above, below, left, right, twist)


def forward(x):
    devices, own_rows, share = x.shape[1:]
    left, right, twist = tables(False)
    vmem = pl.BlockSpec(memory_space=pltpu.VMEM)
    return pl.pallas_call(
        forward_kernel,
        grid=(own_rows // GROUP,),
        in_specs=[pl.BlockSpec((2, devices, GROUP, share), lambda g: (0, 0, g, 0)), vmem, vmem, vmem],
        out_specs=pl.BlockSpec((2, GROUP, FACTOR, FACTOR), lambda g: (0, g, 0, 0)),
        out_shape=jax.ShapeDtypeStruct((2, own_rows, FACTOR, FACTOR), jnp.float32),
        scratch_shapes=[pltpu.VMEM((2, FACTOR * GROUP, FACTOR), jnp.float32)],
        compiler_params=pltpu.CompilerParams(vmem_limit_bytes=40 * 2**20),
    )(x, left, right, twist)


def from_behind(shard, axis, by):
    devices = lax.axis_size(axis)
    pairs = [(i, i + by) for i in range(devices) if 0 <= i + by < devices]
    return lax.ppermute(shard, axis, pairs)


def place_of(centroid, shifts, own_rows):
    block = lax.axis_index("row") * own_rows // BLOCK
    chosen = block == jnp.arange(centroid.shape[0], dtype=jnp.int32)
    return jnp.stack([jnp.sum(jnp.where(chosen, centroid, 0)), jnp.sum(jnp.where(chosen, shifts, 0))])


def per_device(raw_echo, centroid, shifts, chirp_rate):
    devices = lax.axis_size("row")
    own_rows = raw_echo.shape[1] // devices
    share = raw_echo.shape[2]
    assert BLOCK % own_rows == 0 and own_rows % GROUP == 0 and own_rows >= UPPER
    place = place_of(centroid, shifts, own_rows)
    blocks = raw_echo.reshape(2, devices, own_rows, share)
    gathered = lax.all_to_all(blocks, "row", split_axis=1, concat_axis=1, tiled=True)
    spectrum = forward(gathered)
    above = from_behind(spectrum[:, :UPPER], "row", -1)
    below = from_behind(spectrum[:, own_rows - LOWER :], "row", 1)
    return backward(place, chirp_rate, spectrum, above, below)


def solution(mesh):
    return jax.shard_map(
        per_device,
        mesh=mesh,
        in_specs=(P(None, "slab", "row"), P("slab"), P("slab"), P(("slab", "row"))),
        out_specs=P(None, ("slab", "row"), None),
        check_vma=False,
    )
```

profile of v0, /device:TPU:12, one launch (start us, length us, event | category | flops | bytes accessed | tf_op | source)
XLA Modules:
  0.0 161.9 jit_solution(7060736500518428959)
XLA Ops:
  0.0 2.5 %copy.12 = f32[2,16,32,1024]{3,2,0,1:T(8,128)S(1)} copy(f32[2,16,32,1024]{3,2,1,0:T(8,128)} %bitcast.3) | data formatting | bytes 8388608 | tf_op jit(solution)/shard_map/reshape | solution.py:266
  2.5 98.0 %all_to_all.5 = f32[2,16,32,1024]{3,2,0,1:T(8,128)S(1)} all-to-all(f32[2,16,32,1024]{3,2,0,1:T(8,128)S(1)} %copy.12), channel_id=1, replica_groups=mesh['slab'=2,'row'=16] {'row'}, dimensions={1} | all-to-all | bytes 8388608 | tf_op jit(solution)/shard_map/all_to_all | solution.py:267
  100.5 0.3 copy.13.x_ref
  100.8 0.7 copy-done.4
  101.5 0.1 copy-done.5
  101.6 0.0 copy-done.7
  101.6 6.0 %shard_map.100.own_ref = f32[2,32,128,128]{3,2,1,0:T(8,128)S(1)} custom-call(f32[2,16,32,1024]{3,2,1,0:T(8,128)S(1)} %copy.13.x_ref, bf16[256,768]{1,0:T(8,128)(2,1)S(1)} %copy-done.5, bf16[768,256]{1,0:T(8,128)(2,1)S(1)} %copy-done.4, f32[2,128,128]{2,1,0:T(8,128)S(1)} %copy-done.7), custom_call_target="tpu_custom_call" | custom-call | tf_op jit(solution)/shard_map/pallas_call | solution.py:237
  107.6 0.0 copy-start.9
  107.6 0.0 copy-start.10
  107.7 0.0 copy-start.2
  107.7 0.0 copy-start.3
  107.7 0.0 copy-start.6
  107.7 0.0 copy-start.8
  107.7 1.5 slice.8
  109.2 3.0 %collective-permute-start = (f32[2,15,128,128]{3,2,1,0:T(8,128)}, f32[2,15,128,128]{3,2,1,0:T(8,128)S(1)}, u32[]{:S(2)}, u32[]{:S(2)}) collective-permute-start(f32[2,15,128,128]{3,2,1,0:T(8,128)} %slice.8), channel_id=1, source_target_pairs={{1,0},{2,1},{3,2},{4,3},{5,4},{6,5},{7,6},{8,7},{9,8},{10,9},{11,1... | collective-permute-start | bytes 5898248 | tf_op jit(solution)/shard_map/ppermute | solution.py:251
  112.2 0.8 slice.9
  113.0 2.0 %copy-done = f32[2,32,128,128]{3,2,1,0:T(8,128)} copy-done((f32[2,32,128,128]{3,2,1,0:T(8,128)}, f32[2,32,128,128]{3,2,1,0:T(8,128)S(1)}, u32[]{:S(2)}) %copy-start) | copy-done | bytes 4194328
  115.0 1.9 %collective-permute-start.1 = (f32[2,3,128,128]{3,2,1,0:T(8,128)}, f32[2,3,128,128]{3,2,1,0:T(8,128)S(1)}, u32[]{:S(2)}, u32[]{:S(2)}) collective-permute-start(f32[2,3,128,128]{3,2,1,0:T(8,128)} %slice.9), channel_id=1, source_target_pairs={{0,1},{1,2},{2,3},{3,4},{4,5},{5,6},{6,7},{7,8},{8,9},{9,10},{10,1... | collective-permute-start | bytes 1179656 | tf_op jit(solution)/shard_map/ppermute | solution.py:251
  117.0 0.7 fusion
  117.7 1.4 pad_add_fusion.place_ref
  119.1 22.0 %collective-permute-done.1.below_ref = f32[2,3,128,128]{3,2,1,0:T(8,128)S(1)} collective-permute-done((f32[2,3,128,128]{3,2,1,0:T(8,128)}, f32[2,3,128,128]{3,2,1,0:T(8,128)S(1)}, u32[]{:S(2)}, u32[]{:S(2)}) %collective-permute-start.1) | collective-permute-done | bytes 393248 | tf_op jit(solution)/shard_map/ppermute | solution.py:251
  141.1 0.0 copy-start.1
  141.1 2.2 %copy-done.1 = f32[2,32,128,128]{3,2,1,0:T(8,128)S(1)} copy-done((f32[2,32,128,128]{3,2,1,0:T(8,128)S(1)}, f32[2,32,128,128]{3,2,1,0:T(8,128)}, u32[]{:S(2)}) %copy-start.1) | copy-done | bytes 4194328
  143.3 18.6 %shard_map.101 = f32[2,32,16384]{2,1,0:T(8,128)} custom-call(s32[2]{0:T(128)S(1)} %pad_add_fusion.place_ref, f32[32]{0:T(128)S(1)} %copy-done.8, f32[2,32,128,128]{3,2,1,0:T(8,128)S(1)} %copy-done.1, f32[2,15,128,128]{3,2,1,0:T(8,128)S(1)} %collective-permute-done.above_ref, f32[2,3,128,128]{3,2,1,0:T(8,128)S(1)} %collective-permute-done.1.below_ref, ...), custom_call_target="tpu_custom_call" | custom-call | tf_op jit(solution)/shard_map/pallas_call | solution.py:215
  (11 shorter events, 0.0 us)
Async XLA Ops:
  100.5 1.0 copy-start.4
  100.5 1.1 copy-start.5
  100.5 1.1 copy-start.7
  107.6 9.3 %copy-start.9 = (s32[4]{0:T(128)S(1)}, s32[4]{0:T(128)}, u32[]{:S(2)}) copy-start(s32[4]{0:T(128)} %param.11) | copy-start | bytes 52
  107.6 9.3 %copy-start.10 = (s32[4]{0:T(128)S(1)}, s32[4]{0:T(128)}, u32[]{:S(2)}) copy-start(s32[4]{0:T(128)} %param.12) | copy-start | bytes 52
  107.7 33.4 %copy-start.2 = (bf16[768,256]{1,0:T(8,128)(2,1)S(1)}, bf16[768,256]{1,0:T(8,128)(2,1)}, u32[]{:S(2)}) copy-start(bf16[768,256]{1,0:T(8,128)(2,1)} %constant.39.clone.right_ref) | copy-start | bytes 1179652
  107.7 33.4 %copy-start.3 = (bf16[256,768]{1,0:T(8,128)(2,1)S(1)}, bf16[256,768]{1,0:T(8,128)(2,1)}, u32[]{:S(2)}) copy-start(bf16[256,768]{1,0:T(8,128)(2,1)} %constant.38.clone.left_ref) | copy-start | bytes 1179652
  107.7 33.4 %copy-start.6 = (f32[2,128,128]{2,1,0:T(8,128)S(1)}, f32[2,128,128]{2,1,0:T(8,128)}, u32[]{:S(2)}) copy-start(f32[2,128,128]{2,1,0:T(8,128)} %constant.40.clone.twist_ref) | copy-start | bytes 393220
  107.7 33.4 %copy-start.8 = (f32[32]{0:T(128)S(1)}, f32[32]{0:T(128)}, u32[]{:S(2)}) copy-start(f32[32]{0:T(128)} %rates_ref.1) | copy-start | bytes 388
  109.2 31.8 %collective-permute-start = (f32[2,15,128,128]{3,2,1,0:T(8,128)}, f32[2,15,128,128]{3,2,1,0:T(8,128)S(1)}, u32[]{:S(2)}, u32[]{:S(2)}) collective-permute-start(f32[2,15,128,128]{3,2,1,0:T(8,128)} %slice.8), channel_id=1, source_target_pairs={{1,0},{2,1},{3,2},{4,3},{5,4},{6,5},{7,6},{8,7},{9,8},{10,9},{11,1... | collective-permute-start | bytes 5898248 | tf_op jit(solution)/shard_map/ppermute | solution.py:251
  113.0 2.0 %copy-start = (f32[2,32,128,128]{3,2,1,0:T(8,128)}, f32[2,32,128,128]{3,2,1,0:T(8,128)S(1)}, u32[]{:S(2)}) copy-start(f32[2,32,128,128]{3,2,1,0:T(8,128)S(1)} %shard_map.100.own_ref) | copy-start | bytes 12582916
  115.0 26.0 %collective-permute-start.1 = (f32[2,3,128,128]{3,2,1,0:T(8,128)}, f32[2,3,128,128]{3,2,1,0:T(8,128)S(1)}, u32[]{:S(2)}, u32[]{:S(2)}) collective-permute-start(f32[2,3,128,128]{3,2,1,0:T(8,128)} %slice.9), channel_id=1, source_target_pairs={{0,1},{1,2},{2,3},{3,4},{4,5},{5,6},{6,7},{7,8},{8,9},{9,10},{10,1... | collective-permute-start | bytes 1179656 | tf_op jit(solution)/shard_map/ppermute | solution.py:251
  141.1 2.2 %copy-start.1 = (f32[2,32,128,128]{3,2,1,0:T(8,128)S(1)}, f32[2,32,128,128]{3,2,1,0:T(8,128)}, u32[]{:S(2)}) copy-start(f32[2,32,128,128]{3,2,1,0:T(8,128)} %copy-done) | copy-start | bytes 12582916
where the time goes:
time: 163 us; the launch traced here: 162 us
  blocking collectives  98 us (60%)
  Pallas kernels  24.6 us (15%)
  waiting for transfers between devices  22 us (13%)
  local copies, waits for them, and re-layouts  10.2 us (6%)
  starting transfers between devices  4.92 us (3%)
  other arithmetic  2.11 us (1%)
    all_to_all x1, blocking collectives, per_device(): lax.all_to_all(blocks, 'row', split_axis=1, concat_axis=1, tiled=True)  98 us
    ppermute x2, waiting for transfers between devices, from_behind(): return lax.ppermute(shard, axis, pairs)  22 us
    pallas_call x1, Pallas kernels, backward(): pl.pallas_call(backward_kernel, grid=(own_rows // GROUP,), in_specs=[smem...  18.6 us
    pallas_call x1, Pallas kernels, forward(): pl.pallas_call(forward_kernel, grid=(own_rows // GROUP,), in_specs=[pl.Bl...  6.01 us
    unnamed x22, local copies, waits for them, and re-layouts  5.06 us
    ppermute x2, starting transfers between devices, from_behind(): return lax.ppermute(shard, axis, pairs)  4.92 us
  transfers between devices with their start and end apart: 2, of which 1 were waited for; matrix products, arithmetic and copies ran while one was open for 2% of the time, Pallas kernels for 0%

commit v1 on v0

--- a/solution.py
+++ b/solution.py
@@ -77,25 +77,6 @@
         real, imag = turned(product[:FACTOR, lanes], product[FACTOR:, lanes], twist_ref)
         parts.append(jnp.concatenate([real, imag], axis=1))
     return right_product(right_ref, jnp.concatenate(parts, axis=0))
-
-
-def forward_kernel(x_ref, left_ref, right_ref, twist_ref, out_ref, slow):
-    sources = x_ref.shape[1]
-    pieces = x_ref.shape[3] // FACTOR
-    for c in range(2):
-        for d in range(sources):
-            for j in range(pieces):
-                start = (d * pieces + j) * GROUP
-                slow[c, start : start + GROUP, :] = x_ref[c, d, :, j * FACTOR : (j + 1) * FACTOR]
-    for r in range(0, GROUP, 2):
-        rows = [
-            [slow[c, pl.ds(r + k, FACTOR, stride=GROUP), :] for c in range(2)] for k in range(2)
-        ]
-        result = forward_pair(rows, left_ref, right_ref, twist_ref)
-        for k in range(2):
-            part = result[k * FACTOR : (k + 1) * FACTOR]
-            out_ref[0, r + k] = part[:, :FACTOR]
-            out_ref[1, r + k] = part[:, FACTOR:]
 
 
 def half_turns(t):
@@ -182,32 +163,35 @@
 
 
 def backward_kernel(
-    place_ref, rates_ref, own_ref, above_ref, below_ref, left_ref, right_ref, twist_ref,
+    place_ref, rates_ref, wide_ref, left_ref, right_ref, twist_ref,
     out_ref, extended, weights, window, focus, slow, sems,
 ):
     step = pl.program_id(0)
-    own_rows = own_ref.shape[1]
+    steps = extended.shape[1] // GROUP - (LOWER + UPPER) // GROUP
+    lead = GROUP + LOWER + UPPER
+
+    def piece(g):
+        rows = pl.ds(0, lead) if g == 0 else pl.ds(lead + (g - 1) * GROUP, GROUP)
+        return pltpu.make_async_copy(wide_ref.at[:, rows], extended.at[:, rows], sems.at[g])
 
     @pl.when(step == 0)
     def _():
-        copies = [
-            pltpu.make_async_copy(below_ref, extended.at[:, 0:LOWER], sems.at[0]),
-            pltpu.make_async_copy(own_ref, extended.at[:, LOWER : LOWER + own_rows], sems.at[1]),
-            pltpu.make_async_copy(above_ref, extended.at[:, LOWER + own_rows : LOWER + own_rows + UPPER], sems.at[2]),
-        ]
-        for copy in copies:
-            copy.start()
+        for g in range(steps):
+            piece(g).start()
         fill_weights(place_ref[0], place_ref[1], weights, window)
-        for copy in copies:
-            copy.wait()
+
+    for g in range(steps):
+        @pl.when(step == g)
+        def _():
+            piece(g).wait()
 
     base = step * GROUP
     migrate_rows(base, extended, rates_ref, base, weights, window, focus)
     inverse_group(focus, left_ref, right_ref, twist_ref, slow, out_ref)
 
 
-def backward(place, rates, own, above, below):
-    own_rows = own.shape[1]
+def backward(place, rates, wide):
+    own_rows = wide.shape[1] - LOWER - UPPER
     left, right, twist = tables(True)
     vmem = pl.BlockSpec(memory_space=pltpu.VMEM)
     smem = pl.BlockSpec(memory_space=pltpu.SMEM)
@@ -215,7 +199,7 @@
     return pl.pallas_call(
         backward_kernel,
         grid=(own_rows // GROUP,),
-        in_specs=[smem, smem, hbm, hbm, hbm, vmem, vmem, vmem],
+        in_specs=[smem, smem, hbm, vmem, vmem, vmem],
         out_specs=pl.BlockSpec((2, GROUP, PULSES), lambda g: (0, g, 0)),
         out_shape=jax.ShapeDtypeStruct((2, own_rows, PULSES), jnp.float32),
         scratch_shapes=[
@@ -224,31 +208,162 @@
             pltpu.VMEM((2, FACTOR, FACTOR), jnp.float32),
             pltpu.VMEM((GROUP, FACTOR, 2 * FACTOR), jnp.float32),
             pltpu.VMEM((2, FACTOR * GROUP, FACTOR), jnp.float32),
-            pltpu.SemaphoreType.DMA((3,)),
+            pltpu.SemaphoreType.DMA((own_rows // GROUP,)),
         ],
         compiler_params=pltpu.CompilerParams(vmem_limit_bytes=40 * 2**20),
-    )(place, rates, own, above, below, left, right, twist)
-
-
-def forward(x):
-    devices, own_rows, share = x.shape[1:]
+    )(place, rates, wide, left, right, twist)
+
+
+def gather_kernel(
+    devices, raw_ref, left_ref, right_ref, twist_ref, wide_ref,
+    landed, extended, slow, send_sem, recv_sems, self_sem, out_sems, rim_send, rim_recv,
+):
+    me = lax.axis_index("row")
+    own_rows = landed.shape[2]
+    groups = own_rows // GROUP
+    pieces = landed.shape[3] // FACTOR
+
+    barrier = pltpu.get_barrier_semaphore()
+
+    @pl.loop(1, devices)
+    def _(k):
+        pl.semaphore_signal(barrier, inc=1, device_id={"row": (me + k) % devices})
+
+    pl.semaphore_wait(barrier, devices - 1)
+
+    own = pltpu.make_async_copy(raw_ref.at[:, pl.ds(me * own_rows, own_rows)], landed.at[:, me], self_sem)
+    own.start()
+    for g in range(groups):
+        @pl.loop(1, devices)
+        def _(k):
+            peer = (me + k) % devices
+            pltpu.make_async_remote_copy(
+                src_ref=raw_ref.at[:, pl.ds(peer * own_rows + g * GROUP, GROUP)],
+                dst_ref=landed.at[:, me, pl.ds(g * GROUP, GROUP)],
+                send_sem=send_sem,
+                recv_sem=recv_sems.at[g],
+                device_id={"row": peer},
+            ).start()
+
+    @pl.when(me == 0)
+    def _():
+        extended[:, 0:LOWER] = jnp.zeros((2, LOWER, FACTOR, FACTOR), jnp.float32)
+
+    @pl.when(me == devices - 1)
+    def _():
+        extended[:, LOWER + own_rows :] = jnp.zeros((2, UPPER, FACTOR, FACTOR), jnp.float32)
+
+    own.wait()
+
+    def rim_copy(first, count, target, where, slot):
+        return pltpu.make_async_remote_copy(
+            src_ref=extended.at[:, LOWER + first : LOWER + first + count],
+            dst_ref=extended.at[:, where : where + count],
+            send_sem=rim_send.at[slot],
+            recv_sem=rim_recv.at[slot],
+            device_id={"row": target},
+        )
+
+    above = rim_copy(0, UPPER, jnp.maximum(me - 1, 0), LOWER + own_rows, 0)
+    below = rim_copy(own_rows - LOWER, LOWER, jnp.minimum(me + 1, devices - 1), 0, 1)
+
+    def written(g):
+        rows = pl.ds(LOWER + g * GROUP, GROUP)
+        return pltpu.make_async_copy(extended.at[:, rows], wide_ref.at[:, rows], out_sems.at[g])
+
+    def arrive_and_transform(g):
+        chunk = landed.at[:, 0 : devices - 1, pl.ds(g * GROUP, GROUP)]
+        pltpu.make_async_copy(chunk, chunk, recv_sems.at[g]).wait()
+        rows = pl.ds(pl.multiple_of(g * GROUP, GROUP), GROUP)
+        for c in range(2):
+            for d in range(devices):
+                for j in range(pieces):
+                    start = (d * pieces + j) * GROUP
+                    slow[c, start : start + GROUP, :] = landed[c, d, rows, j * FACTOR : (j + 1) * FACTOR]
+        for r in range(0, GROUP, 2):
+            pair = [
+                [slow[c, pl.ds(r + k, FACTOR, stride=GROUP), :] for c in range(2)] for k in range(2)
+            ]
+            result = forward_pair(pair, left_ref, right_ref, twist_ref)
+            for k in range(2):
+                part = result[k * FACTOR : (k + 1) * FACTOR]
+                extended[0, LOWER + g * GROUP + r + k] = part[:, :FACTOR]
+                extended[1, LOWER + g * GROUP + r + k] = part[:, FACTOR:]
+        written(g).start()
+
+    first = -(-UPPER // GROUP)
+
+    @pl.loop(0, first)
+    def _(g):
+        arrive_and_transform(g)
+
+    @pl.when(me > 0)
+    def _():
+        above.start()
+
+    @pl.loop(first, groups)
+    def _(g):
+        arrive_and_transform(g)
+
+    @pl.when(me < devices - 1)
+    def _():
+        below.start()
+
+    everything = landed.at[:, 0 : devices - 1]
+    pltpu.make_async_copy(everything, everything, send_sem).wait()
+
+    @pl.when(me > 0)
+    def _():
+        above.wait_send()
+        below.wait_recv()
+
+    @pl.when(me < devices - 1)
+    def _():
+        below.wait_send()
+        above.wait_recv()
+
+    rims = [
+        pltpu.make_async_copy(extended.at[:, 0:LOWER], wide_ref.at[:, 0:LOWER], out_sems.at[groups]),
+        pltpu.make_async_copy(
+            extended.at[:, LOWER + own_rows :], wide_ref.at[:, LOWER + own_rows :], out_sems.at[groups + 1]
+        ),
+    ]
+    for rim in rims:
+        rim.start()
+    for g in range(groups):
+        written(g).wait()
+    for rim in rims:
+        rim.wait()
+
+
+def gather_forward(raw, devices):
+    own_rows = raw.shape[1] // devices
+    share = raw.shape[2]
+    groups = own_rows // GROUP
+    wide_shape = (2, own_rows + LOWER + UPPER, FACTOR, FACTOR)
     left, right, twist = tables(False)
     vmem = pl.BlockSpec(memory_space=pltpu.VMEM)
+    hbm = pl.BlockSpec(memory_space=pl.ANY)
     return pl.pallas_call(
-        forward_kernel,
-        grid=(own_rows // GROUP,),
-        in_specs=[pl.BlockSpec((2, devices, GROUP, share), lambda g: (0, 0, g, 0)), vmem, vmem, vmem],
-        out_specs=pl.BlockSpec((2, GROUP, FACTOR, FACTOR), lambda g: (0, g, 0, 0)),
-        out_shape=jax.ShapeDtypeStruct((2, own_rows, FACTOR, FACTOR), jnp.float32),
-        scratch_shapes=[pltpu.VMEM((2, FACTOR * GROUP, FACTOR), jnp.float32)],
-        compiler_params=pltpu.CompilerParams(vmem_limit_bytes=40 * 2**20),
-    )(x, left, right, twist)
-
-
-def from_behind(shard, axis, by):
-    devices = lax.axis_size(axis)
-    pairs = [(i, i + by) for i in range(devices) if 0 <= i + by < devices]
-    return lax.ppermute(shard, axis, pairs)
+        functools.partial(gather_kernel, devices),
+        in_specs=[hbm, vmem, vmem, vmem],
+        out_specs=hbm,
+        out_shape=jax.ShapeDtypeStruct(wide_shape, jnp.float32),
+        scratch_shapes=[
+            pltpu.VMEM((2, devices, own_rows, share), jnp.float32),
+            pltpu.VMEM(wide_shape, jnp.float32),
+            pltpu.VMEM((2, FACTOR * GROUP, FACTOR), jnp.float32),
+            pltpu.SemaphoreType.DMA,
+            pltpu.SemaphoreType.DMA((groups,)),
+            pltpu.SemaphoreType.DMA,
+            pltpu.SemaphoreType.DMA((groups + 2,)),
+            pltpu.SemaphoreType.DMA((2,)),
+            pltpu.SemaphoreType.DMA((2,)),
+        ],
+        compiler_params=pltpu.CompilerParams(
+            collective_id=0, has_side_effects=True, vmem_limit_bytes=40 * 2**20
+        ),
+    )(raw, left, right, twist)
 
 
 def place_of(centroid, shifts, own_rows):
@@ -260,15 +375,10 @@
 def per_device(raw_echo, centroid, shifts, chirp_rate):
     devices = lax.axis_size("row")
     own_rows = raw_echo.shape[1] // devices
-    share = raw_echo.shape[2]
     assert BLOCK % own_rows == 0 and own_rows % GROUP == 0 and own_rows >= UPPER
     place = place_of(centroid, shifts, own_rows)
-    blocks = raw_echo.reshape(2, devices, own_rows, share)
-    gathered = lax.all_to_all(blocks, "row", split_axis=1, concat_axis=1, tiled=True)
-    spectrum = forward(gathered)
-    above = from_behind(spectrum[:, :UPPER], "row", -1)
-    below = from_behind(spectrum[:, own_rows - LOWER :], "row", 1)
-    return backward(place, chirp_rate, spectrum, above, below)
+    wide = gather_forward(raw_echo, devices)
+    return backward(place, chirp_rate, wide)
 
 
 def solution(mesh):

time: 163 us -> 148 us (0.908)
  Pallas kernels: 24.6 us -> 140 us
  blocking collectives: 98 us -> 0 us
  waiting for transfers between devices: 22 us -> 0 us
  local copies, waits for them, and re-layouts: 10.2 us -> 5.1 us
  starting transfers between devices: 4.92 us -> 0 us
    pallas_call x1, Pallas kernels: 6.01 us -> 121 us  [gather_forward(): pl.pallas_call(functools.partial(gather_kernel, devices), in_specs=[hbm,...]
    all_to_all x1 -> x0, blocking collectives: 98 us -> none  [per_device(): lax.all_to_all(blocks, 'row', split_axis=1, concat_axis=1, tiled=True)]
    ppermute x2 -> x0, waiting for transfers between devices: 22 us -> none  [from_behind(): return lax.ppermute(shard, axis, pairs)]
    ppermute x2 -> x0, starting transfers between devices: 4.92 us -> none  [from_behind(): return lax.ppermute(shard, axis, pairs)]
    reshape x1 -> x0, local copies, waits for them, and re-layouts: 2.49 us -> none  [per_device(): blocks = raw_echo.reshape(2, devices, own_rows, share)]
    slice x2 -> x0, local copies, waits for them, and re-layouts: 2.3 us -> none  [the longest x1 1.51 us: per_device(): above = from_behind(spectrum[:, :UPPER], 'row', -1)]
    unnamed x22 -> x16, local copies, waits for them, and re-layouts: 5.06 us -> 5.1 us
  transfers between devices with their start and end apart: 2 -> 0, of which waited for: 1 -> 0; matrix products, arithmetic and copies ran while one was open for 2% -> 0% of each run, Pallas kernels for 0% -> 0%
where the time goes in v1:
time: 148 us
  Pallas kernels  140 us (95%)
  local copies, waits for them, and re-layouts  5.1 us (3%)
  other arithmetic  2.67 us (2%)
    pallas_call x1, Pallas kernels, gather_forward(): pl.pallas_call(functools.partial(gather_kernel, devices), in_specs=[hbm,...  121 us
    pallas_call x1, Pallas kernels, backward(): pl.pallas_call(backward_kernel, grid=(own_rows // GROUP,), in_specs=[smem...  18.8 us
    unnamed x16, local copies, waits for them, and re-layouts  5.1 us

profile of v1, /device:TPU:12, one launch (start us, length us, event | category | flops | bytes accessed | tf_op | source)
XLA Modules:
  0.0 147.9 jit_solution(8597768430085608505)
XLA Ops:
  0.0 1.3 fusion
  1.3 1.3 pad_add_fusion.place_ref
  2.7 0.0 copy-start
  2.7 2.2 %copy-done = f32[2,512,1024]{2,1,0:T(8,128)S(1)} copy-done((f32[2,512,1024]{2,1,0:T(8,128)S(1)}, f32[2,512,1024]{2,1,0:T(8,128)}, u32[]{:S(2)}) %copy-start) | copy-done | bytes 4194328
  4.9 0.0 copy-start.3
  4.9 1.0 copy-done.3
  5.9 0.0 copy-start.4
  5.9 1.0 copy-done.4
  6.9 0.0 copy-start.6
  6.9 0.9 copy-done.6
  7.8 0.0 copy-start.1
  7.8 0.0 copy-start.2
  7.8 0.0 copy-start.5
  7.8 0.0 copy-start.7
  7.8 121.2 %shard_map.100.wide_ref = f32[2,50,128,128]{3,2,1,0:T(8,128)S(1)} custom-call(f32[2,512,1024]{2,1,0:T(8,128)S(1)} %copy-done, bf16[256,768]{1,0:T(8,128)(2,1)S(1)} %copy-done.4, bf16[768,256]{1,0:T(8,128)(2,1)S(1)} %copy-done.3, f32[2,128,128]{2,1,0:T(8,128)S(1)} %copy-done.6), custom_call_target="tpu_custom_call" | custom-call | tf_op jit(solution)/shard_map/pallas_call | solution.py:347
  129.0 0.0 copy-done.1
  129.0 0.0 copy-done.2
  129.0 0.0 copy-done.5
  129.0 0.0 copy-done.7
  129.0 18.8 %shard_map.101 = f32[2,32,16384]{2,1,0:T(8,128)} custom-call(s32[2]{0:T(128)S(1)} %pad_add_fusion.place_ref, f32[32]{0:T(128)S(1)} %copy-done.7, f32[2,50,128,128]{3,2,1,0:T(8,128)S(1)} %shard_map.100.wide_ref, bf16[256,768]{1,0:T(8,128)(2,1)S(1)} %copy-done.2, bf16[768,256]{1,0:T(8,128)(2,1)S(1)} %copy-done.1, f32[2,128,128]{2,1,0:T(8,128)S(1)} %copy-done.5), custom_call_target="tpu_custom_call" | custom-call | tf_op jit(solution)/shard_map/pallas_call | solution.py:199
Async XLA Ops:
  2.7 2.2 %copy-start = (f32[2,512,1024]{2,1,0:T(8,128)S(1)}, f32[2,512,1024]{2,1,0:T(8,128)}, u32[]{:S(2)}) copy-start(f32[2,512,1024]{2,1,0:T(8,128)} %raw_ref.1) | copy-start | bytes 12582916
  4.9 1.0 copy-start.3
  5.9 1.0 copy-start.4
  6.9 0.9 copy-start.6
  7.8 121.2 %copy-start.1 = (bf16[768,256]{1,0:T(8,128)(2,1)S(1)}, bf16[768,256]{1,0:T(8,128)(2,1)}, u32[]{:S(2)}) copy-start(bf16[768,256]{1,0:T(8,128)(2,1)} %constant.39.clone.right_ref) | copy-start | bytes 1179652
  7.8 121.2 %copy-start.2 = (bf16[256,768]{1,0:T(8,128)(2,1)S(1)}, bf16[256,768]{1,0:T(8,128)(2,1)}, u32[]{:S(2)}) copy-start(bf16[256,768]{1,0:T(8,128)(2,1)} %constant.38.clone.left_ref) | copy-start | bytes 1179652
  7.8 121.2 %copy-start.5 = (f32[2,128,128]{2,1,0:T(8,128)S(1)}, f32[2,128,128]{2,1,0:T(8,128)}, u32[]{:S(2)}) copy-start(f32[2,128,128]{2,1,0:T(8,128)} %constant.40.clone.twist_ref) | copy-start | bytes 393220
  7.8 121.2 %copy-start.7 = (f32[32]{0:T(128)S(1)}, f32[32]{0:T(128)}, u32[]{:S(2)}) copy-start(f32[32]{0:T(128)} %rates_ref.1) | copy-start | bytes 388

commit v2 on v1

--- a/solution.py
+++ b/solution.py
@@ -163,7 +163,7 @@
 
 
 def backward_kernel(
-    place_ref, rates_ref, wide_ref, left_ref, right_ref, twist_ref,
+    centroid_ref, shifts_ref, rates_ref, wide_ref, left_ref, right_ref, twist_ref,
     out_ref, extended, weights, window, focus, slow, sems,
 ):
     step = pl.program_id(0)
@@ -178,7 +178,8 @@
     def _():
         for g in range(steps):
             piece(g).start()
-        fill_weights(place_ref[0], place_ref[1], weights, window)
+        block = lax.axis_index("row") * rates_ref.shape[0] // BLOCK
+        fill_weights(centroid_ref[block], shifts_ref[block], weights, window)
 
     for g in range(steps):
         @pl.when(step == g)
@@ -190,7 +191,7 @@
     inverse_group(focus, left_ref, right_ref, twist_ref, slow, out_ref)
 
 
-def backward(place, rates, wide):
+def backward(centroid, shifts, rates, wide):
     own_rows = wide.shape[1] - LOWER - UPPER
     left, right, twist = tables(True)
     vmem = pl.BlockSpec(memory_space=pltpu.VMEM)
@@ -199,7 +200,7 @@
     return pl.pallas_call(
         backward_kernel,
         grid=(own_rows // GROUP,),
-        in_specs=[smem, smem, hbm, vmem, vmem, vmem],
+        in_specs=[smem, smem, smem, hbm, vmem, vmem, vmem],
         out_specs=pl.BlockSpec((2, GROUP, PULSES), lambda g: (0, g, 0)),
         out_shape=jax.ShapeDtypeStruct((2, own_rows, PULSES), jnp.float32),
         scratch_shapes=[
@@ -210,19 +211,27 @@
             pltpu.VMEM((2, FACTOR * GROUP, FACTOR), jnp.float32),
             pltpu.SemaphoreType.DMA((own_rows // GROUP,)),
         ],
-        compiler_params=pltpu.CompilerParams(vmem_limit_bytes=40 * 2**20),
-    )(place, rates, wide, left, right, twist)
+        compiler_params=pltpu.CompilerParams(vmem_limit_bytes=60 * 2**20),
+    )(centroid, shifts, rates, wide, left, right, twist)
 
 
 def gather_kernel(
-    devices, raw_ref, left_ref, right_ref, twist_ref, wide_ref,
-    landed, extended, slow, send_sem, recv_sems, self_sem, out_sems, rim_send, rim_recv,
+    devices, raw_ref, left_hbm, right_hbm, twist_hbm, wide_ref,
+    left_ref, right_ref, twist_ref, table_sems, landed, extended, slow, send_sem, recv_sems, self_sem, out_sems, rim_send, rim_recv,
 ):
     me = lax.axis_index("row")
     own_rows = landed.shape[2]
     groups = own_rows // GROUP
     pieces = landed.shape[3] // FACTOR
 
+    fetches = [
+        pltpu.make_async_copy(source, target, table_sems.at[i])
+        for i, (source, target) in enumerate(
+            [(left_hbm, left_ref), (right_hbm, right_ref), (twist_hbm, twist_ref)]
+        )
+    ]
+    for fetch in fetches:
+        fetch.start()
     barrier = pltpu.get_barrier_semaphore()
 
     @pl.loop(1, devices)
@@ -233,7 +242,10 @@
 
     own = pltpu.make_async_copy(raw_ref.at[:, pl.ds(me * own_rows, own_rows)], landed.at[:, me], self_sem)
     own.start()
-    for g in range(groups):
+    first = -(-UPPER // GROUP)
+    order = list(range(first)) + list(range(groups - 1, first - 1, -1))
+
+    def issue(g):
         @pl.loop(1, devices)
         def _(k):
             peer = (me + k) % devices
@@ -245,6 +257,9 @@
                 device_id={"row": peer},
             ).start()
 
+    for g in order[: first + 1]:
+        issue(g)
+
     @pl.when(me == 0)
     def _():
         extended[:, 0:LOWER] = jnp.zeros((2, LOWER, FACTOR, FACTOR), jnp.float32)
@@ -254,6 +269,8 @@
         extended[:, LOWER + own_rows :] = jnp.zeros((2, UPPER, FACTOR, FACTOR), jnp.float32)
 
     own.wait()
+    for fetch in fetches:
+        fetch.wait()
 
     def rim_copy(first, count, target, where, slot):
         return pltpu.make_async_remote_copy(
@@ -291,8 +308,6 @@
                 extended[1, LOWER + g * GROUP + r + k] = part[:, FACTOR:]
         written(g).start()
 
-    first = -(-UPPER // GROUP)
-
     @pl.loop(0, first)
     def _(g):
         arrive_and_transform(g)
@@ -301,13 +316,16 @@
     def _():
         above.start()
 
-    @pl.loop(first, groups)
-    def _(g):
-        arrive_and_transform(g)
-
-    @pl.when(me < devices - 1)
-    def _():
-        below.start()
+    for g in order[first + 1 :]:
+        issue(g)
+
+    @pl.loop(0, groups - first)
+    def _(k):
+        arrive_and_transform(groups - 1 - k)
+
+        @pl.when((k == 0) & (me < devices - 1))
+        def _():
+            below.start()
 
     everything = landed.at[:, 0 : devices - 1]
     pltpu.make_async_copy(everything, everything, send_sem).wait()
@@ -342,14 +360,17 @@
     groups = own_rows // GROUP
     wide_shape = (2, own_rows + LOWER + UPPER, FACTOR, FACTOR)
     left, right, twist = tables(False)
-    vmem = pl.BlockSpec(memory_space=pltpu.VMEM)
     hbm = pl.BlockSpec(memory_space=pl.ANY)
     return pl.pallas_call(
         functools.partial(gather_kernel, devices),
-        in_specs=[hbm, vmem, vmem, vmem],
+        in_specs=[hbm, hbm, hbm, hbm],
         out_specs=hbm,
         out_shape=jax.ShapeDtypeStruct(wide_shape, jnp.float32),
         scratch_shapes=[
+            pltpu.VMEM(left.shape, left.dtype),
+            pltpu.VMEM(right.shape, right.dtype),
+            pltpu.VMEM(twist.shape, twist.dtype),
+            pltpu.SemaphoreType.DMA((3,)),
             pltpu.VMEM((2, devices, own_rows, share), jnp.float32),
             pltpu.VMEM(wide_shape, jnp.float32),
             pltpu.VMEM((2, FACTOR * GROUP, FACTOR), jnp.float32),
@@ -361,24 +382,17 @@
             pltpu.SemaphoreType.DMA((2,)),
         ],
         compiler_params=pltpu.CompilerParams(
-            collective_id=0, has_side_effects=True, vmem_limit_bytes=40 * 2**20
+            collective_id=0, has_side_effects=True, vmem_limit_bytes=58 * 2**20
         ),
     )(raw, left, right, twist)
-
-
-def place_of(centroid, shifts, own_rows):
-    block = lax.axis_index("row") * own_rows // BLOCK
-    chosen = block == jnp.arange(centroid.shape[0], dtype=jnp.int32)
-    return jnp.stack([jnp.sum(jnp.where(chosen, centroid, 0)), jnp.sum(jnp.where(chosen, shifts, 0))])
 
 
 def per_device(raw_echo, centroid, shifts, chirp_rate):
     devices = lax.axis_size("row")
     own_rows = raw_echo.shape[1] // devices
     assert BLOCK % own_rows == 0 and own_rows % GROUP == 0 and own_rows >= UPPER
-    place = place_of(centroid, shifts, own_rows)
     wide = gather_forward(raw_echo, devices)
-    return backward(place, chirp_rate, wide)
+    return backward(centroid, shifts, chirp_rate, wide)
 
 
 def solution(mesh):

time: 148 us -> 140 us (0.946)
  local copies, waits for them, and re-layouts: 5.1 us -> 0 us
  other arithmetic: 2.67 us -> 0 us
    unnamed x16 -> x0, local copies, waits for them, and re-layouts: 5.1 us -> none
where the time goes in v2:
time: 140 us; the launch traced here: 139 us
  Pallas kernels  139 us (99%)
    pallas_call x1, Pallas kernels, gather_forward(): pl.pallas_call(functools.partial(gather_kernel, devices), in_specs=[hbm,...  120 us
    pallas_call x1, Pallas kernels, backward(): pl.pallas_call(backward_kernel, grid=(own_rows // GROUP,), in_specs=[smem...  19.7 us

profile of v2, /device:TPU:12, one launch (start us, length us, event | category | flops | bytes accessed | tf_op | source)
XLA Modules:
  0.0 139.4 jit_solution(6397901541345727757)
XLA Ops:
  0.0 119.7 %shard_map.100.wide_ref = f32[2,50,128,128]{3,2,1,0:T(8,128)} custom-call(f32[2,512,1024]{2,1,0:T(8,128)} %raw_ref.1, bf16[256,768]{1,0:T(8,128)(2,1)} %constant.12.clone.left_hbm, bf16[768,256]{1,0:T(8,128)(2,1)} %constant.13.clone.right_hbm, f32[2,128,128]{2,1,0:T(8,128)} %constant.14.clone.twist_hbm), custom_call_target="tpu_custom_call" | custom-call | tf_op jit(solution)/shard_map/pallas_call | solution.py:364
  119.7 19.7 %shard_map.101 = f32[2,32,16384]{2,1,0:T(8,128)} custom-call(s32[4]{0:T(128)} %centroid_ref.1, s32[4]{0:T(128)} %shifts_ref.1, f32[32]{0:T(128)} %rates_ref.1, f32[2,50,128,128]{3,2,1,0:T(8,128)} %shard_map.100.wide_ref, bf16[256,768]{1,0:T(8,128)(2,1)} %constant.15.clone.left_ref, bf16[768,256]{1,0:T(8,128)(2,1)} %constant.16.clone.right_ref, ...), custom_call_target="tpu_custom_call" | custom-call | tf_op jit(solution)/shard_map/pallas_call | solution.py:200

commit v3 on v2

--- a/solution.py
+++ b/solution.py
@@ -257,7 +257,7 @@
                 device_id={"row": peer},
             ).start()
 
-    for g in order[: first + 1]:
+    for g in order[:first]:
         issue(g)
 
     @pl.when(me == 0)
@@ -316,7 +316,7 @@
     def _():
         above.start()
 
-    for g in order[first + 1 :]:
+    for g in order[first:]:
         issue(g)
 
     @pl.loop(0, groups - first)

time: 140 us -> 142 us (1.014)
  Pallas kernels: 139 us -> 141 us
where the time goes in v3:
time: 142 us; the launch traced here: 141 us
  Pallas kernels  141 us (99%)
    pallas_call x1, Pallas kernels, gather_forward(): pl.pallas_call(functools.partial(gather_kernel, devices), in_specs=[hbm,...  121 us
    pallas_call x1, Pallas kernels, backward(): pl.pallas_call(backward_kernel, grid=(own_rows // GROUP,), in_specs=[smem...  19.7 us

profile of v3, /device:TPU:12, one launch (start us, length us, event | category | flops | bytes accessed | tf_op | source)
XLA Modules:
  0.0 140.8 jit_solution(12114747879643012601)
XLA Ops:
  0.0 121.1 %shard_map.100.wide_ref = f32[2,50,128,128]{3,2,1,0:T(8,128)} custom-call(f32[2,512,1024]{2,1,0:T(8,128)} %raw_ref.1, bf16[256,768]{1,0:T(8,128)(2,1)} %constant.12.clone.left_hbm, bf16[768,256]{1,0:T(8,128)(2,1)} %constant.13.clone.right_hbm, f32[2,128,128]{2,1,0:T(8,128)} %constant.14.clone.twist_hbm), custom_call_target="tpu_custom_call" | custom-call | tf_op jit(solution)/shard_map/pallas_call | solution.py:364
  121.1 19.7 %shard_map.101 = f32[2,32,16384]{2,1,0:T(8,128)} custom-call(s32[4]{0:T(128)} %centroid_ref.1, s32[4]{0:T(128)} %shifts_ref.1, f32[32]{0:T(128)} %rates_ref.1, f32[2,50,128,128]{3,2,1,0:T(8,128)} %shard_map.100.wide_ref, bf16[256,768]{1,0:T(8,128)(2,1)} %constant.15.clone.left_ref, bf16[768,256]{1,0:T(8,128)(2,1)} %constant.16.clone.right_ref, ...), custom_call_target="tpu_custom_call" | custom-call | tf_op jit(solution)/shard_map/pallas_call | solution.py:200
